TPU v7x, 32 devices: a whole 2x2x4 slice. The times are simulated.
32 devices in a mesh: branch: 2 (over x), seq: 16 (over z, y, core).
Axes of the slice: x: 2, y: 2, z: 4, core: 2. Of those that a mesh axis runs over, the one named last changes fastest.
Arguments:
- queries: bfloat16 [8192, 2048], P(('branch', 'seq')), parts along dimension 0, may hold values from -8 to 8
- keys: bfloat16 [8192, 2048], P(('branch', 'seq')), parts along dimension 0, may hold values from -8 to 8
- values: bfloat16 [8192, 2048], P(('branch', 'seq')), parts along dimension 0, may hold values from -6 to 6
- out_grad: bfloat16 [8192, 2048], P(('branch', 'seq')), parts along dimension 0, may hold values from -6 to 6
- segments: int32 [8192], P(('branch', 'seq')), parts along dimension 0, may hold values from 0 to 7, never falling along the last dimension, each value on 1 to 768 neighbouring positions
Outputs:
- attended: bfloat16 [8192, 2048], P(('branch', 'seq')), parts along dimension 0
- query_grad: bfloat16 [8192, 2048], P(('branch', 'seq')), parts along dimension 0
- key_grad: bfloat16 [8192, 2048], P(('branch', 'seq')), parts along dimension 0
- value_grad: bfloat16 [8192, 2048], P(('branch', 'seq')), parts along dimension 0
There are 2 independent parts, one for each index of `branch`. A program takes and returns all parts, laid end to end along the dimension named above; each array names one. Nothing has to cross between parts.
Inputs may be any that keep to these rules, and one draw needn't show every extreme that they name: `segments`: never falling along the sequence; each document has 1 to 768 tokens, and one has exactly 768.
All inputs are finite; a program needn't handle non-finite values.
Results may differ from a plain program's by a relative error of at most 0.017.
Values may be sent and summed in bfloat16 or wider, within the bound.
No kernel may reach another device: no remote copies, remote signals or barrier semaphores. Data moves between devices by JAX's collectives and lax.ppermute only.
A program may use at most 128 MiB of HBM per device.

v0:
```python
import math
from functools import partial

import jax
import jax.numpy as jnp
from jax import lax
from jax.experimental import pallas as pl
from jax.experimental.pallas import tpu as pltpu
from jax.sharding import PartitionSpec as P

HEADS = 16
REACH = 3
FWD_HEADS = 2
FAR_HEADS = 2
HALVES = 2
TILE = 16
HIDE = -1e30


NT = (((1,), (1,)), ((), ()))
TN = (((0,), (0,)), ((), ()))
NN = (((1,), (0,)), ((), ()))


def dot(a, b, dims):
    return lax.dot_general(a, b, dims, preferred_element_type=jnp.float32)


def send(x, pairs):
    peers = lax.axis_size("seq")
    kept = [(i, j) for i, j in pairs if 0 <= j < peers]
    return lax.ppermute(x, "seq", kept)


def fwd_kernel(held, *refs):
    bias, q, g, k0, k1, k2, k3, v0, v1, v2, v3, o, dq, dk, dv, st = refs[held:]
    dim = q.shape[1] // FWD_HEADS
    inv = 1.0 / math.sqrt(dim)
    for h in range(FWD_HEADS):
        cols = slice(h * dim, (h + 1) * dim)
        qh, gh = q[:, cols], g[:, cols]
        ks = [r[:, cols] for r in (k0, k1, k2, k3)]
        vs = [r[:, cols] for r in (v0, v1, v2, v3)]
        s = [dot(k, qh, NT) * inv + bias[b] for b, k in enumerate(ks)]
        peak = jnp.max(s[0], 0, keepdims=True)
        for x in s[1:]:
            peak = jnp.maximum(peak, jnp.max(x, 0, keepdims=True))
        e = [jnp.exp(x - peak) for x in s]
        total = sum(jnp.sum(x, 0, keepdims=True) for x in e)
        recip = 1.0 / total
        w = [(x * recip).astype(jnp.bfloat16) for x in e]
        o[:, cols] = sum(dot(x, v, TN) for x, v in zip(w, vs)).astype(o.dtype)
        dp = [dot(v, gh, NT) for v in vs]
        delta = sum(
            jnp.sum(x.astype(jnp.float32) * y, 0, keepdims=True) for x, y in zip(w, dp)
        )
        ds = [
            (x.astype(jnp.float32) * (y - delta) * inv).astype(jnp.bfloat16)
            for x, y in zip(w, dp)
        ]
        dq[:, cols] = sum(dot(x, k, TN) for x, k in zip(ds, ks)).astype(dq.dtype)
        dk[:, cols] = dot(ds[0], qh, NN)
        dv[:, cols] = dot(w[0], gh, NN)
        st[h, 0:1, :] = peak + jnp.log(total)
        st[h, 1:2, :] = delta


def far_kernel(held, *refs):
    bias, k, v, dk0, dv0, q1, q2, q3, g1, g2, g3, s1, s2, s3, dk, dv = refs[held:]
    dim = k.shape[1] // FAR_HEADS
    inv = 1.0 / math.sqrt(dim)
    for h in range(FAR_HEADS):
        cols = slice(h * dim, (h + 1) * dim)
        kh, vh = k[:, cols], v[:, cols]
        acc_k, acc_v = dk0[:, cols], dv0[:, cols]
        for b, (q, g, st) in enumerate(((q1, g1, s1), (q2, g2, s2), (q3, g3, s3))):
            qh, gh = q[:, cols], g[:, cols]
            s = dot(kh, qh, NT) * inv + bias[b]
            w = jnp.exp(s - st[h, 0:1, :]).astype(jnp.bfloat16)
            dp = dot(vh, gh, NT)
            ds = (w.astype(jnp.float32) * (dp - st[h, 1:2, :]) * inv).astype(jnp.bfloat16)
            acc_k = acc_k + dot(ds, qh, NN)
            acc_v = acc_v + dot(w, gh, NN)
        dk[:, cols] = acc_k.astype(dk.dtype)
        dv[:, cols] = acc_v.astype(dv.dtype)


def pack_kernel(a, b, segs, *refs):
    outs, sems = refs[:HALVES], refs[HALVES]
    half = a.shape[1] // HALVES
    rows = a.shape[0]
    copies = [(segs, outs[0].at[pl.ds(rows, TILE), pl.ds(0, rows)])]
    for n, out in enumerate(outs):
        for m, src in enumerate((a, b)):
            dst = out.at[pl.ds(0, rows), pl.ds(m * half, half)]
            copies.append((src.at[:, pl.ds(n * half, half)], dst))
    copies = [pltpu.make_async_copy(x, y, sems.at[i]) for i, (x, y) in enumerate(copies)]
    for copy in copies:
        copy.start()
    for copy in copies:
        copy.wait()


def local(queries, keys, values, out_grad, segments):
    rows, feature = queries.shape
    dim = feature // HEADS
    half = feature // HALVES
    half_heads = HEADS // HALVES
    peers = lax.axis_size("seq")
    every = range(peers)

    near_up = [(i, i + 1 if i % 2 == 0 else i + 3) for i in every]
    two_up = [(i, i + 2) for i in every]
    near_down = [(i, i - 1 if i % 2 == 1 else i - 3) for i in every]
    two_down = [(i, i - 2) for i in every]
    swap_down = [(i, i - 3 if i % 2 == 1 else i - 1) for i in every]
    swap = [(i, i ^ 1) for i in every]

    own_seg = segments + 1
    seg_rows = jnp.broadcast_to(own_seg.astype(jnp.bfloat16)[None], (TILE, rows))

    def pack(a, b):
        wide = jax.ShapeDtypeStruct((rows, 2 * half), jnp.bfloat16)
        tall = jax.ShapeDtypeStruct((rows + TILE, 2 * half), jnp.bfloat16)
        spec = pl.BlockSpec(memory_space=pl.ANY)
        return pl.pallas_call(
            pack_kernel,
            in_specs=[spec] * 3,
            out_specs=[spec] * HALVES,
            out_shape=[tall] + [wide] * (HALVES - 1),
            scratch_shapes=[pltpu.SemaphoreType.DMA((2 * HALVES + 1,))],
        )(a, b, seg_rows)

    def seg_of(packed):
        return packed[rows, :rows].astype(jnp.int32)

    kv, qg = pack(keys, values), pack(queries, out_grad)
    kv_two, kv_near, qg_near, qg_two, kv_swap, qg_swap = [], [], [], [], [], []
    for n in range(HALVES):
        kv_two.append(send(kv[n], two_up))
        kv_near.append(send(kv[n], near_up))
    for n in range(HALVES):
        qg_near.append(send(qg[n], near_down))
        qg_two.append(send(qg[n], two_down))
    kv_swap.append(send(kv_two[0], swap))

    pos = jnp.arange(rows, dtype=jnp.int32)
    hide = jnp.float32(HIDE)
    key_segs = jnp.stack([own_seg] + [seg_of(x[0]) for x in (kv_near, kv_two, kv_swap)])
    seen = key_segs[:, :, None] == own_seg[None, None, :]
    causal = (pos[:, None] <= pos[None, :])[None] | (jnp.arange(REACH + 1) > 0)[:, None, None]
    bias = jnp.where(seen & causal, 0.0, hide)

    per_fwd, per_far = half // (FWD_HEADS * dim), half // (FAR_HEADS * dim)

    def wide(heads, first):
        return pl.BlockSpec((rows, heads * dim), lambda h: (0, h + first))

    def stat(heads):
        return pl.BlockSpec((heads, 2, rows), lambda h: (h, 0, 0))

    def whole(n):
        return pl.BlockSpec((n, rows, rows), lambda h: (0, 0, 0))

    anywhere = pl.BlockSpec(memory_space=pl.ANY)
    out = jax.ShapeDtypeStruct((rows, feature), jnp.bfloat16)
    part = jax.ShapeDtypeStruct((rows, half), jnp.float32)
    stats = jax.ShapeDtypeStruct((half_heads, 2, rows), jnp.float32)

    def run_fwd(n, before):
        at = n * per_fwd
        own, low, high = wide(FWD_HEADS, at), wide(FWD_HEADS, 0), wide(FWD_HEADS, per_fwd)
        got = (kv_near[n], kv_two[n], kv_swap[n])
        return pl.pallas_call(
            partial(fwd_kernel, len(before)),
            grid=(per_fwd,),
            in_specs=[anywhere] * len(before)
            + [whole(REACH + 1), own, own, own, low, low, low, own, high, high, high],
            out_specs=[own, own, low, low, stat(FWD_HEADS)],
            out_shape=[out, out, part, part, stats],
            input_output_aliases={i: i for i in range(len(before))},
        )(*before, bias, queries, out_grad, keys, *got, values, *got)

    def run_far(n, before, far_bias, dk0, dv0, st):
        at = n * per_far
        own, low, high = wide(FAR_HEADS, at), wide(FAR_HEADS, 0), wide(FAR_HEADS, per_far)
        got = (qg_near[n], qg_two[n], qg_swap[n])
        return pl.pallas_call(
            partial(far_kernel, len(before)),
            grid=(per_far,),
            in_specs=[anywhere] * len(before)
            + [whole(REACH), own, own, low, low, low, low, low, high, high, high]
            + [stat(FAR_HEADS)] * 3,
            out_specs=[own, own],
            out_shape=[out, out],
            input_output_aliases={i: i for i in range(len(before))},
        )(*before, far_bias, keys, values, dk0, dv0, *got, *got, *st)

    before, dk0, dv0, st = (), [], [], []
    for n in range(HALVES):
        if n > 0:
            mine, theirs, _ = lax.optimization_barrier((kv_two[n], kv_near[n], dk0[n - 1]))
            kv_two[n], kv_near[n] = mine, theirs
            kv_swap.append(send(mine, swap))
        *before, a, b, c = run_fwd(n, before)
        dk0.append(a)
        dv0.append(b)
        st.append([send(c, x) for x in (near_down, two_down, swap_down)])
    attended, query_grad = before

    *got, _ = lax.optimization_barrier((*qg_two, *qg_near, dk0[-1]))
    qg_two, qg_near = got[:HALVES], got[HALVES:]
    qg_swap = [send(x, swap) for x in qg_two]
    query_segs = jnp.stack([seg_of(x[0]) for x in (qg_near, qg_two, qg_swap)])
    far_bias = jnp.where(query_segs[:, None, :] == own_seg[None, :, None], 0.0, hide)
    before = ()
    for n in range(HALVES):
        before = run_far(n, before, far_bias, dk0[n], dv0[n], st[n])
    key_grad, value_grad = before
    return attended, query_grad, key_grad, value_grad


def solution(mesh):
    wide = P(("branch", "seq"), None)
    return jax.shard_map(
        local,
        mesh=mesh,
        in_specs=(wide, wide, wide, wide, P(("branch", "seq"))),
        out_specs=(wide, wide, wide, wide),
        check_vma=False,
    )
```

profile of v0, /device:TPU:25, one launch (start us, length us, event | category | flops | bytes accessed | tf_op | source)
XLA Modules:
  0.0 279.9 jit_solution(1274809198362003104)
XLA Ops:
  0.6 0.7 fusion
  1.3 0.6 broadcast_in_dim.16.segs
  1.9 64.9 %shard_map.84 = (bf16[272,2048]{1,0:T(8,128)(2,1)}, bf16[256,2048]{1,0:T(8,128)(2,1)}) custom-call(bf16[256,2048]{1,0:T(8,128)(2,1)} %refs_3_.5, bf16[256,2048]{1,0:T(8,128)(2,1)} %refs_4_.3, bf16[16,256]{1,0:T(8,128)(2,1)} %broadcast_in_dim.16.segs), custom_call_target="tpu_custom_call" | custom-call | tf_op jit(solution)/shard_map/pallas_call | solution.py:126
  66.8 3.1 %collective-permute-start.1 = (bf16[272,2048]{1,0:T(8,128)(2,1)}, bf16[272,2048]{1,0:T(8,128)(2,1)S(1)}, u32[]{:S(2)}, u32[]{:S(2)}) collective-permute-start(bf16[272,2048]{1,0:T(8,128)(2,1)} %get-tuple-element.28), channel_id=1, source_target_pairs={{0,2},{1,3},{2,4},{3,5},{4,6},{5,7},{6,8},{7,9},{8,10},{9,11},{10,... | collective-permute-start | bytes 3342344 | tf_op jit(solution)/shard_map/ppermute | solution.py:32
  70.0 1.3 collective-permute-start
  71.3 24.0 %collective-permute-done.1.refs_5_.refs_9_ = bf16[272,2048]{1,0:T(8,128)(2,1)S(1)} collective-permute-done((bf16[272,2048]{1,0:T(8,128)(2,1)}, bf16[272,2048]{1,0:T(8,128)(2,1)S(1)}, u32[]{:S(2)}, u32[]{:S(2)}) %collective-permute-start.1) | collective-permute-done | bytes 1114144 | tf_op jit(solution)/shard_map/ppermute | solution.py:32
  95.3 2.7 collective-permute-start.2
  98.0 1.9 collective-permute-start.3
  99.9 1.3 collective-permute-start.4
  101.2 64.9 %shard_map.87 = (bf16[272,2048]{1,0:T(8,128)(2,1)}, bf16[256,2048]{1,0:T(8,128)(2,1)}) custom-call(bf16[256,2048]{1,0:T(8,128)(2,1)} %a.3, bf16[256,2048]{1,0:T(8,128)(2,1)} %b.3, bf16[16,256]{1,0:T(8,128)(2,1)} %broadcast_in_dim.16.segs), custom_call_target="tpu_custom_call" | custom-call | tf_op jit(solution)/shard_map/pallas_call | solution.py:126
  166.1 4.9 %collective-permute-start.6 = (bf16[272,2048]{1,0:T(8,128)(2,1)}, bf16[272,2048]{1,0:T(8,128)(2,1)S(1)}, u32[]{:S(2)}, u32[]{:S(2)}) collective-permute-start(bf16[272,2048]{1,0:T(8,128)(2,1)} %get-tuple-element.37), channel_id=1, source_target_pairs={{2,0},{3,1},{4,2},{5,3},{6,4},{7,5},{8,6},{9,7},{10,8},{11,9},{12,... | collective-permute-start | bytes 3342344 | tf_op jit(solution)/shard_map/ppermute | solution.py:32
  171.1 0.0 collective-permute-done.refs_4_.refs_8_
  171.1 2.8 collective-permute-start.8
  173.8 0.7 slice_convert_fusion.2
  174.5 0.0 collective-permute-done.2.refs_6_.refs_10_
  174.5 0.7 slice_convert_fusion
  175.2 1.3 and_select_fusion.refs_0_.refs_2_
  176.5 0.0 copy-done.2
  176.5 14.2 %shard_map.85 = (bf16[256,2048]{1,0:T(8,128)(2,1)}, bf16[256,2048]{1,0:T(8,128)(2,1)}, f32[256,1024]{1,0:T(8,128)}, f32[256,1024]{1,0:T(8,128)}, f32[8,2,256]{2,1,0:T(2,128)}) custom-call(f32[4,256,256]{2,1,0:T(8,128)} %and_select_fusion.refs_0_.refs_2_, bf16[256,2048]{1,0:T(8,128)(2,1)} %a.3, bf16[256,2048]{1,0:T(8,128)(2,1)} %b.3, ...), custom_call_target="tpu_custom_call" | custom-call | tf_op jit(solution)/shard_map/pallas_call | solution.py:174
  190.6 0.0 collective-permute-done.3.refs_7_.refs_11_
  190.6 0.0 collective-permute-done.4.refs_6_.refs_10_
  190.7 1.2 collective-permute-start.5
  191.9 1.9 collective-permute-start.7
  193.8 3.2 %collective-permute-start.9 = (bf16[256,2048]{1,0:T(8,128)(2,1)}, bf16[256,2048]{1,0:T(8,128)(2,1)}, u32[]{:S(2)}, u32[]{:S(2)}) collective-permute-start(bf16[256,2048]{1,0:T(8,128)(2,1)} %get-tuple-element.38), channel_id=1, source_target_pairs={{1,0},{3,2},{4,1},{5,4},{6,3},{7,6},{8,5},{9,8},{10,7},{11,10},{12... | collective-permute-start | bytes 3145736 | tf_op jit(solution)/shard_map/ppermute | solution.py:32
  197.0 0.0 collective-permute-done.5.refs_8_.refs_12_
  197.0 14.2 %shard_map.86 = (bf16[256,2048]{1,0:T(8,128)(2,1)}, bf16[256,2048]{1,0:T(8,128)(2,1)}, f32[256,1024]{1,0:T(8,128)}, f32[256,1024]{1,0:T(8,128)}, f32[8,2,256]{2,1,0:T(2,128)}) custom-call(bf16[256,2048]{1,0:T(8,128)(2,1)} %get-tuple-element.29.refs_0_, bf16[256,2048]{1,0:T(8,128)(2,1)} %get-tuple-element.30.refs_1_, ...), custom_call_target="tpu_custom_call", output_to_operand_aliasing={{0}: (0, {}), {1}: (1, {})} | custom-call | tf_op jit(solution)/shard_map/pallas_call | solution.py:174
  211.2 7.5 %collective-permute-done.7.refs_8_.refs_11_ = bf16[256,2048]{1,0:T(8,128)(2,1)S(1)} collective-permute-done((bf16[256,2048]{1,0:T(8,128)(2,1)}, bf16[256,2048]{1,0:T(8,128)(2,1)S(1)}, u32[]{:S(2)}, u32[]{:S(2)}) %collective-permute-start.7) | collective-permute-done | bytes 1048608 | tf_op jit(solution)/shard_map/ppermute | solution.py:32
  218.7 0.0 collective-permute-done.9.refs_7_.refs_10_
  218.7 0.0 collective-permute-done.6.refs_6_.refs_9_
  218.7 0.0 copy-start
  218.7 0.0 collective-permute-done.8.refs_5_.refs_8_
  218.7 0.9 copy-done.4
  219.7 22.1 %collective-permute-start.10 = (bf16[272,2048]{1,0:T(8,128)(2,1)S(1)}, bf16[272,2048]{1,0:T(8,128)(2,1)S(1)}, u32[]{:S(2)}, u32[]{:S(2)}) collective-permute-start(bf16[272,2048]{1,0:T(8,128)(2,1)S(1)} %collective-permute-done.6.refs_6_.refs_9_), channel_id=1, source_target_pairs={{0,1},{1,0},{2,3},{3,2},{4,5},{5,4},{6,7},{7,6},{8,9},{9,8},{10,11... | collective-permute-start | bytes 3342344 | tf_op jit(solution)/shard_map/ppermute | solution.py:32
  241.8 0.1 collective-permute-start.14
  241.9 0.0 copy-done.11
  241.9 2.3 collective-permute-start.11
  244.2 1.9 collective-permute-start.12
  246.2 6.3 %collective-permute-start.13 = (f32[8,2,256]{2,1,0:T(2,128)S(1)}, f32[8,2,256]{2,1,0:T(2,128)S(1)}, u32[]{:S(2)}, u32[]{:S(2)}) collective-permute-start(f32[8,2,256]{2,1,0:T(2,128)S(1)} %copy-done.11), channel_id=1, source_target_pairs={{2,1},{3,0},{4,3},{5,2},{6,5},{7,4},{8,7},{9,6},{10,9},{11,8},{12,... | collective-permute-start | bytes 49160 | tf_op jit(solution)/shard_map/ppermute | solution.py:32
  252.5 0.0 collective-permute-done.10.refs_7_.refs_10_
  252.5 0.0 copy-start.3
  252.5 1.3 collective-permute-start.15
  253.8 0.0 collective-permute-done.11.refs_11_
  253.8 0.0 copy-start.6
  253.8 2.7 collective-permute-start.16
  256.5 0.0 collective-permute-done.12.refs_12_
  256.5 0.0 copy-start.7
  256.5 3.3 %collective-permute-start.17 = (f32[8,2,256]{2,1,0:T(2,128)}, f32[8,2,256]{2,1,0:T(2,128)S(1)}, u32[]{:S(2)}, u32[]{:S(2)}) collective-permute-start(f32[8,2,256]{2,1,0:T(2,128)} %get-tuple-element.49), channel_id=1, source_target_pairs={{2,1},{3,0},{4,3},{5,2},{6,5},{7,4},{8,7},{9,6},{10,9},{11,8},{12,... | collective-permute-start | bytes 49160 | tf_op jit(solution)/shard_map/ppermute | solution.py:32
  259.8 1.0 compare_select_fusion.refs_0_.refs_2_
  260.8 0.0 collective-permute-done.13.refs_13_
  260.8 0.0 copy-done
  260.8 0.0 copy-done.1
  260.8 0.0 copy-done.3
  260.8 0.0 copy-done.6
  260.8 0.6 copy-done.9
  261.4 8.9 %shard_map.88 = (bf16[256,2048]{1,0:T(8,128)(2,1)}, bf16[256,2048]{1,0:T(8,128)(2,1)}) custom-call(f32[3,256,256]{2,1,0:T(8,128)} %compare_select_fusion.refs_0_.refs_2_, bf16[256,2048]{1,0:T(8,128)(2,1)} %refs_3_.5, bf16[256,2048]{1,0:T(8,128)(2,1)} %refs_4_.3, f32[256,1024]{1,0:T(8,128)} %get-tuple-element.32.refs_3_, ...), custom_call_target="tpu_custom_call" | custom-call | tf_op jit(solution)/shard_map/pallas_call | solution.py:188
  270.3 0.0 collective-permute-done.15.refs_13_
  270.3 0.0 copy-start.5
  270.3 0.0 collective-permute-done.16.refs_14_
  270.3 0.0 collective-permute-done.17.refs_15_
  270.4 0.0 collective-permute-done.14.refs_9_.refs_12_
  270.4 0.5 copy-done.5
  270.9 0.0 copy-done.8
  270.9 0.0 copy-done.10
  271.0 8.9 %shard_map.89 = (bf16[256,2048]{1,0:T(8,128)(2,1)}, bf16[256,2048]{1,0:T(8,128)(2,1)}) custom-call(bf16[256,2048]{1,0:T(8,128)(2,1)} %get-tuple-element.44.refs_0_, bf16[256,2048]{1,0:T(8,128)(2,1)} %get-tuple-element.45.refs_1_, f32[3,256,256]{2,1,0:T(8,128)} %compare_select_fusion.refs_0_.refs_2_, ...), custom_call_target="tpu_custom_call", output_to_operand_aliasing={{0}: (0, {}), {1}: (1, {})} | custom-call | tf_op jit(solution)/shard_map/pallas_call | solution.py:188
  (16 shorter events, 0.1 us)
Async XLA Ops:
  66.8 28.5 %collective-permute-start.1 = (bf16[272,2048]{1,0:T(8,128)(2,1)}, bf16[272,2048]{1,0:T(8,128)(2,1)S(1)}, u32[]{:S(2)}, u32[]{:S(2)}) collective-permute-start(bf16[272,2048]{1,0:T(8,128)(2,1)} %get-tuple-element.28), channel_id=1, source_target_pairs={{0,2},{1,3},{2,4},{3,5},{4,6},{5,7},{6,8},{7,9},{8,10},{9,11},{10,... | collective-permute-start | bytes 3342344 | tf_op jit(solution)/shard_map/ppermute | solution.py:32
  70.0 101.1 %collective-permute-start = (bf16[272,2048]{1,0:T(8,128)(2,1)}, bf16[272,2048]{1,0:T(8,128)(2,1)}, u32[]{:S(2)}, u32[]{:S(2)}) collective-permute-start(bf16[272,2048]{1,0:T(8,128)(2,1)} %get-tuple-element.28), channel_id=1, source_target_pairs={{0,1},{1,4},{2,3},{3,6},{4,5},{5,8},{6,7},{7,10},{8,9},{9,12},{10,... | collective-permute-start | bytes 3342344 | tf_op jit(solution)/shard_map/ppermute | solution.py:32
  95.3 81.2 %copy-start.2 = (bf16[272,2048]{1,0:T(8,128)(2,1)}, bf16[272,2048]{1,0:T(8,128)(2,1)S(1)}, u32[]{:S(2)}) copy-start(bf16[272,2048]{1,0:T(8,128)(2,1)S(1)} %collective-permute-done.1.refs_5_.refs_9_) | copy-start | bytes 3342340
  95.3 79.2 %collective-permute-start.2 = (bf16[272,2048]{1,0:T(8,128)(2,1)S(1)}, bf16[272,2048]{1,0:T(8,128)(2,1)}, u32[]{:S(2)}, u32[]{:S(2)}) collective-permute-start(bf16[272,2048]{1,0:T(8,128)(2,1)S(1)} %collective-permute-done.1.refs_5_.refs_9_), channel_id=1, source_target_pairs={{0,1},{1,0},{2,3},{3,2},{4,5},{5,4},{6,7},{7,6},{8,9},{9,8},{10,11... | collective-permute-start | bytes 3342344 | tf_op jit(solution)/shard_map/ppermute | solution.py:32
  98.0 92.7 %collective-permute-start.3 = (bf16[256,2048]{1,0:T(8,128)(2,1)}, bf16[256,2048]{1,0:T(8,128)(2,1)}, u32[]{:S(2)}, u32[]{:S(2)}) collective-permute-start(bf16[256,2048]{1,0:T(8,128)(2,1)} %get-tuple-element.31), channel_id=1, source_target_pairs={{0,2},{1,3},{2,4},{3,5},{4,6},{5,7},{6,8},{7,9},{8,10},{9,11},{10,... | collective-permute-start | bytes 3145736 | tf_op jit(solution)/shard_map/ppermute | solution.py:32
  99.9 90.8 %collective-permute-start.4 = (bf16[256,2048]{1,0:T(8,128)(2,1)}, bf16[256,2048]{1,0:T(8,128)(2,1)}, u32[]{:S(2)}, u32[]{:S(2)}) collective-permute-start(bf16[256,2048]{1,0:T(8,128)(2,1)} %get-tuple-element.31), channel_id=1, source_target_pairs={{0,1},{1,4},{2,3},{3,6},{4,5},{5,8},{6,7},{7,10},{8,9},{9,12},{10,... | collective-permute-start | bytes 3145736 | tf_op jit(solution)/shard_map/ppermute | solution.py:32
  166.1 52.6 %collective-permute-start.6 = (bf16[272,2048]{1,0:T(8,128)(2,1)}, bf16[272,2048]{1,0:T(8,128)(2,1)S(1)}, u32[]{:S(2)}, u32[]{:S(2)}) collective-permute-start(bf16[272,2048]{1,0:T(8,128)(2,1)} %get-tuple-element.37), channel_id=1, source_target_pairs={{2,0},{3,1},{4,2},{5,3},{6,4},{7,5},{8,6},{9,7},{10,8},{11,9},{12,... | collective-permute-start | bytes 3342344 | tf_op jit(solution)/shard_map/ppermute | solution.py:32
  171.1 47.6 %collective-permute-start.8 = (bf16[272,2048]{1,0:T(8,128)(2,1)}, bf16[272,2048]{1,0:T(8,128)(2,1)S(1)}, u32[]{:S(2)}, u32[]{:S(2)}) collective-permute-start(bf16[272,2048]{1,0:T(8,128)(2,1)} %get-tuple-element.37), channel_id=1, source_target_pairs={{1,0},{3,2},{4,1},{5,4},{6,3},{7,6},{8,5},{9,8},{10,7},{11,10},{12... | collective-permute-start | bytes 3342344 | tf_op jit(solution)/shard_map/ppermute | solution.py:32
  190.7 6.4 %collective-permute-start.5 = (bf16[256,2048]{1,0:T(8,128)(2,1)}, bf16[256,2048]{1,0:T(8,128)(2,1)}, u32[]{:S(2)}, u32[]{:S(2)}) collective-permute-start(bf16[256,2048]{1,0:T(8,128)(2,1)} %collective-permute-done.3.refs_7_.refs_11_), channel_id=1, source_target_pairs={{0,1},{1,0},{2,3},{3,2},{4,5},{5,4},{6,7},{7,6},{8,9},{9,8},{10,11... | collective-permute-start | bytes 3145736 | tf_op jit(solution)/shard_map/ppermute | solution.py:32
  191.9 26.8 %collective-permute-start.7 = (bf16[256,2048]{1,0:T(8,128)(2,1)}, bf16[256,2048]{1,0:T(8,128)(2,1)S(1)}, u32[]{:S(2)}, u32[]{:S(2)}) collective-permute-start(bf16[256,2048]{1,0:T(8,128)(2,1)} %get-tuple-element.38), channel_id=1, source_target_pairs={{2,0},{3,1},{4,2},{5,3},{6,4},{7,5},{8,6},{9,7},{10,8},{11,9},{12,... | collective-permute-start | bytes 3145736 | tf_op jit(solution)/shard_map/ppermute | solution.py:32
  193.8 24.9 %collective-permute-start.9 = (bf16[256,2048]{1,0:T(8,128)(2,1)}, bf16[256,2048]{1,0:T(8,128)(2,1)}, u32[]{:S(2)}, u32[]{:S(2)}) collective-permute-start(bf16[256,2048]{1,0:T(8,128)(2,1)} %get-tuple-element.38), channel_id=1, source_target_pairs={{1,0},{3,2},{4,1},{5,4},{6,3},{7,6},{8,5},{9,8},{10,7},{11,10},{12... | collective-permute-start | bytes 3145736 | tf_op jit(solution)/shard_map/ppermute | solution.py:32
  197.0 44.9 %copy-start.11 = (f32[8,2,256]{2,1,0:T(2,128)S(1)}, f32[8,2,256]{2,1,0:T(2,128)}, u32[]{:S(2)}) copy-start(f32[8,2,256]{2,1,0:T(2,128)} %get-tuple-element.43) | copy-start | bytes 49156
  218.7 1.0 copy-start.4
  218.7 42.1 %copy-start = (bf16[272,2048]{1,0:T(8,128)(2,1)}, bf16[272,2048]{1,0:T(8,128)(2,1)S(1)}, u32[]{:S(2)}) copy-start(bf16[272,2048]{1,0:T(8,128)(2,1)S(1)} %collective-permute-done.6.refs_6_.refs_9_) | copy-start | bytes 3342340
  219.7 41.1 %copy-start.1 = (bf16[272,2048]{1,0:T(8,128)(2,1)}, bf16[272,2048]{1,0:T(8,128)(2,1)S(1)}, u32[]{:S(2)}) copy-start(bf16[272,2048]{1,0:T(8,128)(2,1)S(1)} %collective-permute-done.8.refs_5_.refs_8_) | copy-start | bytes 3342340
  219.7 32.8 %collective-permute-start.10 = (bf16[272,2048]{1,0:T(8,128)(2,1)S(1)}, bf16[272,2048]{1,0:T(8,128)(2,1)S(1)}, u32[]{:S(2)}, u32[]{:S(2)}) collective-permute-start(bf16[272,2048]{1,0:T(8,128)(2,1)S(1)} %collective-permute-done.6.refs_6_.refs_9_), channel_id=1, source_target_pairs={{0,1},{1,0},{2,3},{3,2},{4,5},{5,4},{6,7},{7,6},{8,9},{9,8},{10,11... | collective-permute-start | bytes 3342344 | tf_op jit(solution)/shard_map/ppermute | solution.py:32
  241.8 28.5 %collective-permute-start.14 = (bf16[256,2048]{1,0:T(8,128)(2,1)}, bf16[256,2048]{1,0:T(8,128)(2,1)}, u32[]{:S(2)}, u32[]{:S(2)}) collective-permute-start(bf16[256,2048]{1,0:T(8,128)(2,1)} %copy-done.4), channel_id=1, source_target_pairs={{0,1},{1,0},{2,3},{3,2},{4,5},{5,4},{6,7},{7,6},{8,9},{9,8},{10,11... | collective-permute-start | bytes 3145736 | tf_op jit(solution)/shard_map/ppermute | solution.py:32
  241.9 11.9 %collective-permute-start.11 = (f32[8,2,256]{2,1,0:T(2,128)S(1)}, f32[8,2,256]{2,1,0:T(2,128)S(1)}, u32[]{:S(2)}, u32[]{:S(2)}) collective-permute-start(f32[8,2,256]{2,1,0:T(2,128)S(1)} %copy-done.11), channel_id=1, source_target_pairs={{1,0},{3,2},{4,1},{5,4},{6,3},{7,6},{8,5},{9,8},{10,7},{11,10},{12... | collective-permute-start | bytes 49160 | tf_op jit(solution)/shard_map/ppermute | solution.py:32
  244.2 12.3 %collective-permute-start.12 = (f32[8,2,256]{2,1,0:T(2,128)S(1)}, f32[8,2,256]{2,1,0:T(2,128)S(1)}, u32[]{:S(2)}, u32[]{:S(2)}) collective-permute-start(f32[8,2,256]{2,1,0:T(2,128)S(1)} %copy-done.11), channel_id=1, source_target_pairs={{2,0},{3,1},{4,2},{5,3},{6,4},{7,5},{8,6},{9,7},{10,8},{11,9},{12,... | collective-permute-start | bytes 49160 | tf_op jit(solution)/shard_map/ppermute | solution.py:32
  246.2 14.6 %collective-permute-start.13 = (f32[8,2,256]{2,1,0:T(2,128)S(1)}, f32[8,2,256]{2,1,0:T(2,128)S(1)}, u32[]{:S(2)}, u32[]{:S(2)}) collective-permute-start(f32[8,2,256]{2,1,0:T(2,128)S(1)} %copy-done.11), channel_id=1, source_target_pairs={{2,1},{3,0},{4,3},{5,2},{6,5},{7,4},{8,7},{9,6},{10,9},{11,8},{12,... | collective-permute-start | bytes 49160 | tf_op jit(solution)/shard_map/ppermute | solution.py:32
  252.5 8.3 %copy-start.3 = (bf16[272,2048]{1,0:T(8,128)(2,1)}, bf16[272,2048]{1,0:T(8,128)(2,1)S(1)}, u32[]{:S(2)}) copy-start(bf16[272,2048]{1,0:T(8,128)(2,1)S(1)} %collective-permute-done.10.refs_7_.refs_10_) | copy-start | bytes 3342340
  252.5 17.8 %collective-permute-start.15 = (f32[8,2,256]{2,1,0:T(2,128)}, f32[8,2,256]{2,1,0:T(2,128)S(1)}, u32[]{:S(2)}, u32[]{:S(2)}) collective-permute-start(f32[8,2,256]{2,1,0:T(2,128)} %get-tuple-element.49), channel_id=1, source_target_pairs={{1,0},{3,2},{4,1},{5,4},{6,3},{7,6},{8,5},{9,8},{10,7},{11,10},{12... | collective-permute-start | bytes 49160 | tf_op jit(solution)/shard_map/ppermute | solution.py:32
  253.8 7.0 %copy-start.6 = (f32[8,2,256]{2,1,0:T(2,128)}, f32[8,2,256]{2,1,0:T(2,128)S(1)}, u32[]{:S(2)}) copy-start(f32[8,2,256]{2,1,0:T(2,128)S(1)} %collective-permute-done.11.refs_11_) | copy-start | bytes 49156
  253.8 16.5 %collective-permute-start.16 = (f32[8,2,256]{2,1,0:T(2,128)}, f32[8,2,256]{2,1,0:T(2,128)S(1)}, u32[]{:S(2)}, u32[]{:S(2)}) collective-permute-start(f32[8,2,256]{2,1,0:T(2,128)} %get-tuple-element.49), channel_id=1, source_target_pairs={{2,0},{3,1},{4,2},{5,3},{6,4},{7,5},{8,6},{9,7},{10,8},{11,9},{12,... | collective-permute-start | bytes 49160 | tf_op jit(solution)/shard_map/ppermute | solution.py:32
  256.5 4.3 %copy-start.7 = (f32[8,2,256]{2,1,0:T(2,128)}, f32[8,2,256]{2,1,0:T(2,128)S(1)}, u32[]{:S(2)}) copy-start(f32[8,2,256]{2,1,0:T(2,128)S(1)} %collective-permute-done.12.refs_12_) | copy-start | bytes 49156
  256.5 13.8 %collective-permute-start.17 = (f32[8,2,256]{2,1,0:T(2,128)}, f32[8,2,256]{2,1,0:T(2,128)S(1)}, u32[]{:S(2)}, u32[]{:S(2)}) collective-permute-start(f32[8,2,256]{2,1,0:T(2,128)} %get-tuple-element.49), channel_id=1, source_target_pairs={{2,1},{3,0},{4,3},{5,2},{6,5},{7,4},{8,7},{9,6},{10,9},{11,8},{12,... | collective-permute-start | bytes 49160 | tf_op jit(solution)/shard_map/ppermute | solution.py:32
  260.8 0.6 copy-start.9
  270.3 0.6 copy-start.5
  270.3 0.6 copy-start.8
  270.4 0.6 copy-start.10
where the time goes:
time: 281 us; the launch traced here: 280 us
  Pallas kernels  176 us (63%)
  starting transfers between devices  64.2 us (23%)
  waiting for transfers between devices  31.5 us (11%)
  other arithmetic  4.36 us (2%)
    pallas_call x2, Pallas kernels, pack(): pl.pallas_call(pack_kernel, in_specs=[spec] * 3, out_specs=[spec] * HALVE...  130 us
    ppermute x18, starting transfers between devices, send(): return lax.ppermute(x, 'seq', kept)  64.2 us
    ppermute x18, waiting for transfers between devices, send(): return lax.ppermute(x, 'seq', kept)  31.5 us
    pallas_call x2, Pallas kernels, run_fwd(): pl.pallas_call(partial(fwd_kernel, len(before)), grid=(per_fwd,), in_spec...  28.3 us
    pallas_call x2, Pallas kernels, run_far(): pl.pallas_call(partial(far_kernel, len(before)), grid=(per_far,), in_spec...  17.8 us
  transfers between devices with their start and end apart: 18, of which 2 were waited for; matrix products, arithmetic and copies ran while one was open for 1% of the time, Pallas kernels for 36%

commit v1 on v0

--- a/solution.py
+++ b/solution.py
@@ -5,7 +5,6 @@
 import jax.numpy as jnp
 from jax import lax
 from jax.experimental import pallas as pl
-from jax.experimental.pallas import tpu as pltpu
 from jax.sharding import PartitionSpec as P
 
 HEADS = 16
@@ -85,20 +84,16 @@
         dv[:, cols] = acc_v.astype(dv.dtype)
 
 
-def pack_kernel(a, b, segs, *refs):
-    outs, sems = refs[:HALVES], refs[HALVES]
-    half = a.shape[1] // HALVES
-    rows = a.shape[0]
-    copies = [(segs, outs[0].at[pl.ds(rows, TILE), pl.ds(0, rows)])]
-    for n, out in enumerate(outs):
-        for m, src in enumerate((a, b)):
-            dst = out.at[pl.ds(0, rows), pl.ds(m * half, half)]
-            copies.append((src.at[:, pl.ds(n * half, half)], dst))
-    copies = [pltpu.make_async_copy(x, y, sems.at[i]) for i, (x, y) in enumerate(copies)]
-    for copy in copies:
-        copy.start()
-    for copy in copies:
-        copy.wait()
+def pack_kernel(a, b, segs, *outs):
+    half, rows = a.shape[1] // HALVES, a.shape[0]
+    for m, src in enumerate((a, b)):
+
+        @pl.when(pl.program_id(0) == m)
+        def _(src=src):
+            for n, out in enumerate(outs):
+                out[:rows, :] = src[:, n * half : (n + 1) * half]
+            outs[0][rows:, :rows] = segs[...]
+            outs[0][rows:, rows:] = jnp.zeros((TILE, half - rows), jnp.bfloat16)
 
 
 def local(queries, keys, values, out_grad, segments):
@@ -122,13 +117,14 @@
     def pack(a, b):
         wide = jax.ShapeDtypeStruct((rows, 2 * half), jnp.bfloat16)
         tall = jax.ShapeDtypeStruct((rows + TILE, 2 * half), jnp.bfloat16)
-        spec = pl.BlockSpec(memory_space=pl.ANY)
+        full = pl.BlockSpec((rows, feature), lambda m: (0, 0))
         return pl.pallas_call(
             pack_kernel,
-            in_specs=[spec] * 3,
-            out_specs=[spec] * HALVES,
+            grid=(2,),
+            in_specs=[full, full, pl.BlockSpec((TILE, rows), lambda m: (0, 0))],
+            out_specs=[pl.BlockSpec((rows + TILE, half), lambda m: (0, m))]
+            + [pl.BlockSpec((rows, half), lambda m: (0, m))] * (HALVES - 1),
             out_shape=[tall] + [wide] * (HALVES - 1),
-            scratch_shapes=[pltpu.SemaphoreType.DMA((2 * HALVES + 1,))],
         )(a, b, seg_rows)
 
     def seg_of(packed):
@@ -205,16 +201,21 @@
         *before, a, b, c = run_fwd(n, before)
         dk0.append(a)
         dv0.append(b)
-        st.append([send(c, x) for x in (near_down, two_down, swap_down)])
+        ways = (near_down, two_down, swap_down)
+        st.append([send(c, x) for x in ways])
     attended, query_grad = before
 
-    *got, _ = lax.optimization_barrier((*qg_two, *qg_near, dk0[-1]))
-    qg_two, qg_near = got[:HALVES], got[HALVES:]
-    qg_swap = [send(x, swap) for x in qg_two]
+    def swap_qg(n, after):
+        qg_two[n], qg_near[n], _ = lax.optimization_barrier((qg_two[n], qg_near[n], after))
+        qg_swap.append(send(qg_two[n], swap))
+
+    swap_qg(0, dk0[-1])
     query_segs = jnp.stack([seg_of(x[0]) for x in (qg_near, qg_two, qg_swap)])
     far_bias = jnp.where(query_segs[:, None, :] == own_seg[None, :, None], 0.0, hide)
     before = ()
     for n in range(HALVES):
+        if n > 0:
+            swap_qg(n, before[0])
         before = run_far(n, before, far_bias, dk0[n], dv0[n], st[n])
     key_grad, value_grad = before
     return attended, query_grad, key_grad, value_grad

time: 281 us -> 176 us (0.63)
  Pallas kernels: 176 us -> 52.1 us
  waiting for transfers between devices: 31.5 us -> 47.6 us
    pallas_call x2, Pallas kernels: 130 us -> 5.96 us  [pack(): pl.pallas_call(pack_kernel, grid=(2,), in_specs=[full, full, pl.BlockSpec...]
    ppermute x18, waiting for transfers between devices: 31.5 us -> 47.6 us  [send(): return lax.ppermute(x, 'seq', kept)]
  transfers between devices with their start and end apart: 18 -> 18, of which waited for: 2 -> 7; matrix products, arithmetic and copies ran while one was open for 1% -> 2% of each run, Pallas kernels for 36% -> 23%
where the time goes in v1:
time: 176 us; the launch traced here: 175 us
  starting transfers between devices  66.8 us (38%)
  Pallas kernels  52.1 us (30%)
  waiting for transfers between devices  47.6 us (27%)
  other arithmetic  4.36 us (2%)
  local copies, waits for them, and re-layouts  3.18 us (2%)
    ppermute x18, starting transfers between devices, send(): return lax.ppermute(x, 'seq', kept)  66.8 us
    ppermute x18, waiting for transfers between devices, send(): return lax.ppermute(x, 'seq', kept)  47.6 us
    pallas_call x2, Pallas kernels, run_fwd(): pl.pallas_call(partial(fwd_kernel, len(before)), grid=(per_fwd,), in_spec...  28.3 us
    pallas_call x2, Pallas kernels, run_far(): pl.pallas_call(partial(far_kernel, len(before)), grid=(per_far,), in_spec...  17.8 us
    pallas_call x2, Pallas kernels, pack(): pl.pallas_call(pack_kernel, grid=(2,), in_specs=[full, full, pl.BlockSpec...  5.96 us
  transfers between devices with their start and end apart: 18, of which 7 were waited for; matrix products, arithmetic and copies ran while one was open for 2% of the time, Pallas kernels for 23%

profile of v1, /device:TPU:25, one launch (start us, length us, event | category | flops | bytes accessed | tf_op | source)
XLA Modules:
  0.0 174.9 jit_solution(10841453944928237300)
XLA Ops:
  0.6 0.7 fusion
  1.3 0.6 broadcast_in_dim.16.segs
  1.9 3.0 %shard_map.84 = (bf16[272,2048]{1,0:T(8,128)(2,1)}, bf16[256,2048]{1,0:T(8,128)(2,1)}) custom-call(bf16[256,2048]{1,0:T(8,128)(2,1)} %refs_3_.5, bf16[256,2048]{1,0:T(8,128)(2,1)} %refs_4_.3, bf16[16,256]{1,0:T(8,128)(2,1)} %broadcast_in_dim.16.segs), custom_call_target="tpu_custom_call" | custom-call | tf_op jit(solution)/shard_map/pallas_call | solution.py:121
  4.9 3.1 %collective-permute-start.1 = (bf16[272,2048]{1,0:T(8,128)(2,1)}, bf16[272,2048]{1,0:T(8,128)(2,1)S(1)}, u32[]{:S(2)}, u32[]{:S(2)}) collective-permute-start(bf16[272,2048]{1,0:T(8,128)(2,1)} %get-tuple-element.28), channel_id=1, source_target_pairs={{0,2},{1,3},{2,4},{3,5},{4,6},{5,7},{6,8},{7,9},{8,10},{9,11},{10,... | collective-permute-start | bytes 3342344 | tf_op jit(solution)/shard_map/ppermute | solution.py:31
  8.0 1.3 collective-permute-start
  9.3 24.0 %collective-permute-done.1.refs_5_.refs_9_ = bf16[272,2048]{1,0:T(8,128)(2,1)S(1)} collective-permute-done((bf16[272,2048]{1,0:T(8,128)(2,1)}, bf16[272,2048]{1,0:T(8,128)(2,1)S(1)}, u32[]{:S(2)}, u32[]{:S(2)}) %collective-permute-start.1) | collective-permute-done | bytes 1114144 | tf_op jit(solution)/shard_map/ppermute | solution.py:31
  33.3 2.7 %collective-permute-start.2 = (bf16[272,2048]{1,0:T(8,128)(2,1)S(1)}, bf16[272,2048]{1,0:T(8,128)(2,1)}, u32[]{:S(2)}, u32[]{:S(2)}) collective-permute-start(bf16[272,2048]{1,0:T(8,128)(2,1)S(1)} %collective-permute-done.1.refs_5_.refs_9_), channel_id=1, source_target_pairs={{0,1},{1,0},{2,3},{3,2},{4,5},{5,4},{6,7},{7,6},{8,9},{9,8},{10,11... | collective-permute-start | bytes 3342344 | tf_op jit(solution)/shard_map/ppermute | solution.py:31
  36.0 1.9 %collective-permute-start.3 = (bf16[256,2048]{1,0:T(8,128)(2,1)}, bf16[256,2048]{1,0:T(8,128)(2,1)}, u32[]{:S(2)}, u32[]{:S(2)}) collective-permute-start(bf16[256,2048]{1,0:T(8,128)(2,1)} %get-tuple-element.31), channel_id=1, source_target_pairs={{0,2},{1,3},{2,4},{3,5},{4,6},{5,7},{6,8},{7,9},{8,10},{9,11},{10,... | collective-permute-start | bytes 3145736 | tf_op jit(solution)/shard_map/ppermute | solution.py:31
  37.9 1.3 collective-permute-start.4
  39.2 3.0 %shard_map.87 = (bf16[272,2048]{1,0:T(8,128)(2,1)}, bf16[256,2048]{1,0:T(8,128)(2,1)}) custom-call(bf16[256,2048]{1,0:T(8,128)(2,1)} %a.3, bf16[256,2048]{1,0:T(8,128)(2,1)} %b.3, bf16[16,256]{1,0:T(8,128)(2,1)} %broadcast_in_dim.16.segs), custom_call_target="tpu_custom_call" | custom-call | tf_op jit(solution)/shard_map/pallas_call | solution.py:121
  42.2 4.9 %collective-permute-start.6 = (bf16[272,2048]{1,0:T(8,128)(2,1)}, bf16[272,2048]{1,0:T(8,128)(2,1)S(1)}, u32[]{:S(2)}, u32[]{:S(2)}) collective-permute-start(bf16[272,2048]{1,0:T(8,128)(2,1)} %get-tuple-element.37), channel_id=1, source_target_pairs={{2,0},{3,1},{4,2},{5,3},{6,4},{7,5},{8,6},{9,7},{10,8},{11,9},{12,... | collective-permute-start | bytes 3342344 | tf_op jit(solution)/shard_map/ppermute | solution.py:31
  47.1 0.0 collective-permute-done.refs_4_.refs_8_
  47.2 2.8 %collective-permute-start.7 = (bf16[272,2048]{1,0:T(8,128)(2,1)}, bf16[272,2048]{1,0:T(8,128)(2,1)S(1)}, u32[]{:S(2)}, u32[]{:S(2)}) collective-permute-start(bf16[272,2048]{1,0:T(8,128)(2,1)} %get-tuple-element.37), channel_id=1, source_target_pairs={{1,0},{3,2},{4,1},{5,4},{6,3},{7,6},{8,5},{9,8},{10,7},{11,10},{12... | collective-permute-start | bytes 3342344 | tf_op jit(solution)/shard_map/ppermute | solution.py:31
  49.9 0.7 slice_convert_fusion.2
  50.6 0.0 collective-permute-done.2.refs_6_.refs_10_
  50.6 0.7 slice_convert_fusion
  51.3 1.3 and_select_fusion.refs_0_.refs_2_
  52.6 0.0 copy-done.2
  52.6 14.1 %shard_map.85 = (bf16[256,2048]{1,0:T(8,128)(2,1)}, bf16[256,2048]{1,0:T(8,128)(2,1)}, f32[256,1024]{1,0:T(8,128)}, f32[256,1024]{1,0:T(8,128)}, f32[8,2,256]{2,1,0:T(2,128)}) custom-call(f32[4,256,256]{2,1,0:T(8,128)} %and_select_fusion.refs_0_.refs_2_, bf16[256,2048]{1,0:T(8,128)(2,1)} %a.3, bf16[256,2048]{1,0:T(8,128)(2,1)} %b.3, ...), custom_call_target="tpu_custom_call" | custom-call | tf_op jit(solution)/shard_map/pallas_call | solution.py:170
  66.7 2.1 %collective-permute-done.3.refs_7_.refs_11_ = bf16[256,2048]{1,0:T(8,128)(2,1)} collective-permute-done((bf16[256,2048]{1,0:T(8,128)(2,1)}, bf16[256,2048]{1,0:T(8,128)(2,1)}, u32[]{:S(2)}, u32[]{:S(2)}) %collective-permute-start.3) | collective-permute-done | bytes 1048608 | tf_op jit(solution)/shard_map/ppermute | solution.py:31
  68.8 0.0 collective-permute-done.4.refs_6_.refs_10_
  68.8 0.0 collective-permute-start.5
  68.8 2.9 %collective-permute-done.5.refs_8_.refs_12_ = bf16[256,2048]{1,0:T(8,128)(2,1)S(1)} collective-permute-done((bf16[256,2048]{1,0:T(8,128)(2,1)}, bf16[256,2048]{1,0:T(8,128)(2,1)S(1)}, u32[]{:S(2)}, u32[]{:S(2)}) %collective-permute-start.5) | collective-permute-done | bytes 1048608 | tf_op jit(solution)/shard_map/ppermute | solution.py:31
  71.6 1.0 copy-done.5
  72.6 14.2 %shard_map.86 = (bf16[256,2048]{1,0:T(8,128)(2,1)}, bf16[256,2048]{1,0:T(8,128)(2,1)}, f32[256,1024]{1,0:T(8,128)}, f32[256,1024]{1,0:T(8,128)}, f32[8,2,256]{2,1,0:T(2,128)}) custom-call(bf16[256,2048]{1,0:T(8,128)(2,1)} %get-tuple-element.29.refs_0_, bf16[256,2048]{1,0:T(8,128)(2,1)} %get-tuple-element.30.refs_1_, ...), custom_call_target="tpu_custom_call", output_to_operand_aliasing={{0}: (0, {}), {1}: (1, {})} | custom-call | tf_op jit(solution)/shard_map/pallas_call | solution.py:170
  86.8 3.3 %collective-permute-done.6.refs_6_.refs_9_ = bf16[272,2048]{1,0:T(8,128)(2,1)S(1)} collective-permute-done((bf16[272,2048]{1,0:T(8,128)(2,1)}, bf16[272,2048]{1,0:T(8,128)(2,1)S(1)}, u32[]{:S(2)}, u32[]{:S(2)}) %collective-permute-start.6) | collective-permute-done | bytes 1114144 | tf_op jit(solution)/shard_map/ppermute | solution.py:31
  90.1 0.0 collective-permute-done.7.refs_5_.refs_8_
  90.1 1.3 collective-permute-start.8
  91.4 16.2 %collective-permute-start.12 = (bf16[256,2048]{1,0:T(8,128)(2,1)}, bf16[256,2048]{1,0:T(8,128)(2,1)}, u32[]{:S(2)}, u32[]{:S(2)}) collective-permute-start(bf16[256,2048]{1,0:T(8,128)(2,1)} %get-tuple-element.46), channel_id=1, source_target_pairs={{2,0},{3,1},{4,2},{5,3},{6,4},{7,5},{8,6},{9,7},{10,8},{11,9},{12,... | collective-permute-start | bytes 3145736 | tf_op jit(solution)/shard_map/ppermute | solution.py:31
  107.5 3.3 %collective-permute-start.13 = (bf16[256,2048]{1,0:T(8,128)(2,1)}, bf16[256,2048]{1,0:T(8,128)(2,1)}, u32[]{:S(2)}, u32[]{:S(2)}) collective-permute-start(bf16[256,2048]{1,0:T(8,128)(2,1)} %get-tuple-element.46), channel_id=1, source_target_pairs={{1,0},{3,2},{4,1},{5,4},{6,3},{7,6},{8,5},{9,8},{10,7},{11,10},{12... | collective-permute-start | bytes 3145736 | tf_op jit(solution)/shard_map/ppermute | solution.py:31
  110.9 0.0 copy-done.13
  110.9 1.9 %collective-permute-start.10 = (f32[8,2,256]{2,1,0:T(2,128)S(1)}, f32[8,2,256]{2,1,0:T(2,128)S(1)}, u32[]{:S(2)}, u32[]{:S(2)}) collective-permute-start(f32[8,2,256]{2,1,0:T(2,128)S(1)} %copy-done.13), channel_id=1, source_target_pairs={{2,0},{3,1},{4,2},{5,3},{6,4},{7,5},{8,6},{9,7},{10,8},{11,9},{12,... | collective-permute-start | bytes 49160 | tf_op jit(solution)/shard_map/ppermute | solution.py:31
  112.8 2.5 %collective-permute-start.11 = (f32[8,2,256]{2,1,0:T(2,128)S(1)}, f32[8,2,256]{2,1,0:T(2,128)S(1)}, u32[]{:S(2)}, u32[]{:S(2)}) collective-permute-start(f32[8,2,256]{2,1,0:T(2,128)S(1)} %copy-done.13), channel_id=1, source_target_pairs={{2,1},{3,0},{4,3},{5,2},{6,5},{7,4},{8,7},{9,6},{10,9},{11,8},{12,... | collective-permute-start | bytes 49160 | tf_op jit(solution)/shard_map/ppermute | solution.py:31
  115.3 0.0 collective-permute-done.8.refs_7_.refs_10_
  115.3 0.0 copy-start.3
  115.3 2.1 %collective-permute-start.9 = (f32[8,2,256]{2,1,0:T(2,128)S(1)}, f32[8,2,256]{2,1,0:T(2,128)S(1)}, u32[]{:S(2)}, u32[]{:S(2)}) collective-permute-start(f32[8,2,256]{2,1,0:T(2,128)S(1)} %copy-done.13), channel_id=1, source_target_pairs={{1,0},{3,2},{4,1},{5,4},{6,3},{7,6},{8,5},{9,8},{10,7},{11,10},{12... | collective-permute-start | bytes 49160 | tf_op jit(solution)/shard_map/ppermute | solution.py:31
  117.5 1.0 compare_select_fusion.refs_0_.refs_2_
  118.5 12.0 %collective-permute-done.10.refs_12_ = f32[8,2,256]{2,1,0:T(2,128)S(1)} collective-permute-done((f32[8,2,256]{2,1,0:T(2,128)S(1)}, f32[8,2,256]{2,1,0:T(2,128)S(1)}, u32[]{:S(2)}, u32[]{:S(2)}) %collective-permute-start.10) | collective-permute-done | bytes 16416 | tf_op jit(solution)/shard_map/ppermute | solution.py:31
  130.5 0.3 collective-permute-done.11.refs_13_
  130.8 0.0 collective-permute-done.9.refs_11_
  130.8 0.0 copy-done
  130.8 0.0 copy-done.1
  130.8 0.0 copy-done.3
  130.8 0.2 copy-done.6
  131.1 0.4 copy-done.7
  131.4 0.0 copy-done.10
  131.4 8.9 %shard_map.88 = (bf16[256,2048]{1,0:T(8,128)(2,1)}, bf16[256,2048]{1,0:T(8,128)(2,1)}) custom-call(f32[3,256,256]{2,1,0:T(8,128)} %compare_select_fusion.refs_0_.refs_2_, bf16[256,2048]{1,0:T(8,128)(2,1)} %refs_3_.5, bf16[256,2048]{1,0:T(8,128)(2,1)} %refs_4_.3, f32[256,1024]{1,0:T(8,128)} %get-tuple-element.32.refs_3_, ...), custom_call_target="tpu_custom_call" | custom-call | tf_op jit(solution)/shard_map/pallas_call | solution.py:184
  140.3 0.0 collective-permute-done.12.refs_8_.refs_11_
  140.3 0.0 collective-permute-done.13.refs_7_.refs_10_
  140.4 12.5 %collective-permute-start.14 = (bf16[256,2048]{1,0:T(8,128)(2,1)}, bf16[256,2048]{1,0:T(8,128)(2,1)S(1)}, u32[]{:S(2)}, u32[]{:S(2)}) collective-permute-start(bf16[256,2048]{1,0:T(8,128)(2,1)} %collective-permute-done.12.refs_8_.refs_11_), channel_id=1, source_target_pairs={{0,1},{1,0},{2,3},{3,2},{4,5},{5,4},{6,7},{7,6},{8,9},{9,8},{10,11... | collective-permute-start | bytes 3145736 | tf_op jit(solution)/shard_map/ppermute | solution.py:31
  152.8 0.0 copy-done.12
  152.8 1.9 %collective-permute-start.15 = (f32[8,2,256]{2,1,0:T(2,128)S(1)}, f32[8,2,256]{2,1,0:T(2,128)S(1)}, u32[]{:S(2)}, u32[]{:S(2)}) collective-permute-start(f32[8,2,256]{2,1,0:T(2,128)S(1)} %copy-done.12), channel_id=1, source_target_pairs={{1,0},{3,2},{4,1},{5,4},{6,3},{7,6},{8,5},{9,8},{10,7},{11,10},{12... | collective-permute-start | bytes 49160 | tf_op jit(solution)/shard_map/ppermute | solution.py:31
  154.8 4.8 %collective-permute-start.16 = (f32[8,2,256]{2,1,0:T(2,128)S(1)}, f32[8,2,256]{2,1,0:T(2,128)S(1)}, u32[]{:S(2)}, u32[]{:S(2)}) collective-permute-start(f32[8,2,256]{2,1,0:T(2,128)S(1)} %copy-done.12), channel_id=1, source_target_pairs={{2,0},{3,1},{4,2},{5,3},{6,4},{7,5},{8,6},{9,7},{10,8},{11,9},{12,... | collective-permute-start | bytes 49160 | tf_op jit(solution)/shard_map/ppermute | solution.py:31
  159.5 2.5 %collective-permute-start.17 = (f32[8,2,256]{2,1,0:T(2,128)S(1)}, f32[8,2,256]{2,1,0:T(2,128)S(1)}, u32[]{:S(2)}, u32[]{:S(2)}) collective-permute-start(f32[8,2,256]{2,1,0:T(2,128)S(1)} %copy-done.12), channel_id=1, source_target_pairs={{2,1},{3,0},{4,3},{5,2},{6,5},{7,4},{8,7},{9,6},{10,9},{11,8},{12,... | collective-permute-start | bytes 49160 | tf_op jit(solution)/shard_map/ppermute | solution.py:31
  162.0 0.0 collective-permute-done.15.refs_13_
  162.0 0.0 copy-start.8
  162.0 0.0 collective-permute-done.16.refs_14_
  162.1 0.0 copy-start.9
  162.1 2.9 %collective-permute-done.17.refs_15_ = f32[8,2,256]{2,1,0:T(2,128)S(1)} collective-permute-done((f32[8,2,256]{2,1,0:T(2,128)S(1)}, f32[8,2,256]{2,1,0:T(2,128)S(1)}, u32[]{:S(2)}, u32[]{:S(2)}) %collective-permute-start.17) | collective-permute-done | bytes 16416 | tf_op jit(solution)/shard_map/ppermute | solution.py:31
  165.0 0.0 collective-permute-done.14.refs_9_.refs_12_
  165.0 0.0 copy-done.8
  165.0 0.6 copy-done.11
  165.6 0.4 copy-done.4
  166.0 8.9 %shard_map.89 = (bf16[256,2048]{1,0:T(8,128)(2,1)}, bf16[256,2048]{1,0:T(8,128)(2,1)}) custom-call(bf16[256,2048]{1,0:T(8,128)(2,1)} %get-tuple-element.43.refs_0_, bf16[256,2048]{1,0:T(8,128)(2,1)} %get-tuple-element.44.refs_1_, f32[3,256,256]{2,1,0:T(8,128)} %compare_select_fusion.refs_0_.refs_2_, ...), custom_call_target="tpu_custom_call", output_to_operand_aliasing={{0}: (0, {}), {1}: (1, {})} | custom-call | tf_op jit(solution)/shard_map/pallas_call | solution.py:184
  (20 shorter events, 0.1 us)
Async XLA Ops:
  4.9 28.4 %collective-permute-start.1 = (bf16[272,2048]{1,0:T(8,128)(2,1)}, bf16[272,2048]{1,0:T(8,128)(2,1)S(1)}, u32[]{:S(2)}, u32[]{:S(2)}) collective-permute-start(bf16[272,2048]{1,0:T(8,128)(2,1)} %get-tuple-element.28), channel_id=1, source_target_pairs={{0,2},{1,3},{2,4},{3,5},{4,6},{5,7},{6,8},{7,9},{8,10},{9,11},{10,... | collective-permute-start | bytes 3342344 | tf_op jit(solution)/shard_map/ppermute | solution.py:31
  8.0 39.1 %collective-permute-start = (bf16[272,2048]{1,0:T(8,128)(2,1)}, bf16[272,2048]{1,0:T(8,128)(2,1)}, u32[]{:S(2)}, u32[]{:S(2)}) collective-permute-start(bf16[272,2048]{1,0:T(8,128)(2,1)} %get-tuple-element.28), channel_id=1, source_target_pairs={{0,1},{1,4},{2,3},{3,6},{4,5},{5,8},{6,7},{7,10},{8,9},{9,12},{10,... | collective-permute-start | bytes 3342344 | tf_op jit(solution)/shard_map/ppermute | solution.py:31
  33.3 19.2 %copy-start.2 = (bf16[272,2048]{1,0:T(8,128)(2,1)}, bf16[272,2048]{1,0:T(8,128)(2,1)S(1)}, u32[]{:S(2)}) copy-start(bf16[272,2048]{1,0:T(8,128)(2,1)S(1)} %collective-permute-done.1.refs_5_.refs_9_) | copy-start | bytes 3342340
  33.3 17.3 %collective-permute-start.2 = (bf16[272,2048]{1,0:T(8,128)(2,1)S(1)}, bf16[272,2048]{1,0:T(8,128)(2,1)}, u32[]{:S(2)}, u32[]{:S(2)}) collective-permute-start(bf16[272,2048]{1,0:T(8,128)(2,1)S(1)} %collective-permute-done.1.refs_5_.refs_9_), channel_id=1, source_target_pairs={{0,1},{1,0},{2,3},{3,2},{4,5},{5,4},{6,7},{7,6},{8,9},{9,8},{10,11... | collective-permute-start | bytes 3342344 | tf_op jit(solution)/shard_map/ppermute | solution.py:31
  36.0 32.8 %collective-permute-start.3 = (bf16[256,2048]{1,0:T(8,128)(2,1)}, bf16[256,2048]{1,0:T(8,128)(2,1)}, u32[]{:S(2)}, u32[]{:S(2)}) collective-permute-start(bf16[256,2048]{1,0:T(8,128)(2,1)} %get-tuple-element.31), channel_id=1, source_target_pairs={{0,2},{1,3},{2,4},{3,5},{4,6},{5,7},{6,8},{7,9},{8,10},{9,11},{10,... | collective-permute-start | bytes 3145736 | tf_op jit(solution)/shard_map/ppermute | solution.py:31
  37.9 30.9 %collective-permute-start.4 = (bf16[256,2048]{1,0:T(8,128)(2,1)}, bf16[256,2048]{1,0:T(8,128)(2,1)}, u32[]{:S(2)}, u32[]{:S(2)}) collective-permute-start(bf16[256,2048]{1,0:T(8,128)(2,1)} %get-tuple-element.31), channel_id=1, source_target_pairs={{0,1},{1,4},{2,3},{3,6},{4,5},{5,8},{6,7},{7,10},{8,9},{9,12},{10,... | collective-permute-start | bytes 3145736 | tf_op jit(solution)/shard_map/ppermute | solution.py:31
  42.2 47.9 %collective-permute-start.6 = (bf16[272,2048]{1,0:T(8,128)(2,1)}, bf16[272,2048]{1,0:T(8,128)(2,1)S(1)}, u32[]{:S(2)}, u32[]{:S(2)}) collective-permute-start(bf16[272,2048]{1,0:T(8,128)(2,1)} %get-tuple-element.37), channel_id=1, source_target_pairs={{2,0},{3,1},{4,2},{5,3},{6,4},{7,5},{8,6},{9,7},{10,8},{11,9},{12,... | collective-permute-start | bytes 3342344 | tf_op jit(solution)/shard_map/ppermute | solution.py:31
  47.2 43.0 %collective-permute-start.7 = (bf16[272,2048]{1,0:T(8,128)(2,1)}, bf16[272,2048]{1,0:T(8,128)(2,1)S(1)}, u32[]{:S(2)}, u32[]{:S(2)}) collective-permute-start(bf16[272,2048]{1,0:T(8,128)(2,1)} %get-tuple-element.37), channel_id=1, source_target_pairs={{1,0},{3,2},{4,1},{5,4},{6,3},{7,6},{8,5},{9,8},{10,7},{11,10},{12... | collective-permute-start | bytes 3342344 | tf_op jit(solution)/shard_map/ppermute | solution.py:31
  68.8 2.9 %collective-permute-start.5 = (bf16[256,2048]{1,0:T(8,128)(2,1)}, bf16[256,2048]{1,0:T(8,128)(2,1)S(1)}, u32[]{:S(2)}, u32[]{:S(2)}) collective-permute-start(bf16[256,2048]{1,0:T(8,128)(2,1)} %collective-permute-done.3.refs_7_.refs_11_), channel_id=1, source_target_pairs={{0,1},{1,0},{2,3},{3,2},{4,5},{5,4},{6,7},{7,6},{8,9},{9,8},{10,11... | collective-permute-start | bytes 3145736 | tf_op jit(solution)/shard_map/ppermute | solution.py:31
  71.6 1.0 copy-start.5
  72.6 38.3 %copy-start.13 = (f32[8,2,256]{2,1,0:T(2,128)S(1)}, f32[8,2,256]{2,1,0:T(2,128)}, u32[]{:S(2)}) copy-start(f32[8,2,256]{2,1,0:T(2,128)} %get-tuple-element.42) | copy-start | bytes 49156
  90.1 40.7 %copy-start = (bf16[272,2048]{1,0:T(8,128)(2,1)}, bf16[272,2048]{1,0:T(8,128)(2,1)S(1)}, u32[]{:S(2)}) copy-start(bf16[272,2048]{1,0:T(8,128)(2,1)S(1)} %collective-permute-done.6.refs_6_.refs_9_) | copy-start | bytes 3342340
  90.1 40.7 %copy-start.1 = (bf16[272,2048]{1,0:T(8,128)(2,1)}, bf16[272,2048]{1,0:T(8,128)(2,1)S(1)}, u32[]{:S(2)}) copy-start(bf16[272,2048]{1,0:T(8,128)(2,1)S(1)} %collective-permute-done.7.refs_5_.refs_8_) | copy-start | bytes 3342340
  90.1 25.2 %collective-permute-start.8 = (bf16[272,2048]{1,0:T(8,128)(2,1)S(1)}, bf16[272,2048]{1,0:T(8,128)(2,1)S(1)}, u32[]{:S(2)}, u32[]{:S(2)}) collective-permute-start(bf16[272,2048]{1,0:T(8,128)(2,1)S(1)} %collective-permute-done.6.refs_6_.refs_9_), channel_id=1, source_target_pairs={{0,1},{1,0},{2,3},{3,2},{4,5},{5,4},{6,7},{7,6},{8,9},{9,8},{10,11... | collective-permute-start | bytes 3342344 | tf_op jit(solution)/shard_map/ppermute | solution.py:31
  91.4 49.0 %collective-permute-start.12 = (bf16[256,2048]{1,0:T(8,128)(2,1)}, bf16[256,2048]{1,0:T(8,128)(2,1)}, u32[]{:S(2)}, u32[]{:S(2)}) collective-permute-start(bf16[256,2048]{1,0:T(8,128)(2,1)} %get-tuple-element.46), channel_id=1, source_target_pairs={{2,0},{3,1},{4,2},{5,3},{6,4},{7,5},{8,6},{9,7},{10,8},{11,9},{12,... | collective-permute-start | bytes 3145736 | tf_op jit(solution)/shard_map/ppermute | solution.py:31
  107.5 32.8 %collective-permute-start.13 = (bf16[256,2048]{1,0:T(8,128)(2,1)}, bf16[256,2048]{1,0:T(8,128)(2,1)}, u32[]{:S(2)}, u32[]{:S(2)}) collective-permute-start(bf16[256,2048]{1,0:T(8,128)(2,1)} %get-tuple-element.46), channel_id=1, source_target_pairs={{1,0},{3,2},{4,1},{5,4},{6,3},{7,6},{8,5},{9,8},{10,7},{11,10},{12... | collective-permute-start | bytes 3145736 | tf_op jit(solution)/shard_map/ppermute | solution.py:31
  110.9 19.6 %collective-permute-start.10 = (f32[8,2,256]{2,1,0:T(2,128)S(1)}, f32[8,2,256]{2,1,0:T(2,128)S(1)}, u32[]{:S(2)}, u32[]{:S(2)}) collective-permute-start(f32[8,2,256]{2,1,0:T(2,128)S(1)} %copy-done.13), channel_id=1, source_target_pairs={{2,0},{3,1},{4,2},{5,3},{6,4},{7,5},{8,6},{9,7},{10,8},{11,9},{12,... | collective-permute-start | bytes 49160 | tf_op jit(solution)/shard_map/ppermute | solution.py:31
  112.8 18.0 %collective-permute-start.11 = (f32[8,2,256]{2,1,0:T(2,128)S(1)}, f32[8,2,256]{2,1,0:T(2,128)S(1)}, u32[]{:S(2)}, u32[]{:S(2)}) collective-permute-start(f32[8,2,256]{2,1,0:T(2,128)S(1)} %copy-done.13), channel_id=1, source_target_pairs={{2,1},{3,0},{4,3},{5,2},{6,5},{7,4},{8,7},{9,6},{10,9},{11,8},{12,... | collective-permute-start | bytes 49160 | tf_op jit(solution)/shard_map/ppermute | solution.py:31
  115.3 15.5 %copy-start.3 = (bf16[272,2048]{1,0:T(8,128)(2,1)}, bf16[272,2048]{1,0:T(8,128)(2,1)S(1)}, u32[]{:S(2)}) copy-start(bf16[272,2048]{1,0:T(8,128)(2,1)S(1)} %collective-permute-done.8.refs_7_.refs_10_) | copy-start | bytes 3342340
  115.3 15.5 %collective-permute-start.9 = (f32[8,2,256]{2,1,0:T(2,128)S(1)}, f32[8,2,256]{2,1,0:T(2,128)S(1)}, u32[]{:S(2)}, u32[]{:S(2)}) collective-permute-start(f32[8,2,256]{2,1,0:T(2,128)S(1)} %copy-done.13), channel_id=1, source_target_pairs={{1,0},{3,2},{4,1},{5,4},{6,3},{7,6},{8,5},{9,8},{10,7},{11,10},{12... | collective-permute-start | bytes 49160 | tf_op jit(solution)/shard_map/ppermute | solution.py:31
  130.5 0.6 copy-start.6
  130.8 0.6 copy-start.7
  130.8 0.6 copy-start.10
  131.4 21.4 %copy-start.12 = (f32[8,2,256]{2,1,0:T(2,128)S(1)}, f32[8,2,256]{2,1,0:T(2,128)}, u32[]{:S(2)}) copy-start(f32[8,2,256]{2,1,0:T(2,128)} %get-tuple-element.49) | copy-start | bytes 49156
  140.4 24.6 %collective-permute-start.14 = (bf16[256,2048]{1,0:T(8,128)(2,1)}, bf16[256,2048]{1,0:T(8,128)(2,1)S(1)}, u32[]{:S(2)}, u32[]{:S(2)}) collective-permute-start(bf16[256,2048]{1,0:T(8,128)(2,1)} %collective-permute-done.12.refs_8_.refs_11_), channel_id=1, source_target_pairs={{0,1},{1,0},{2,3},{3,2},{4,5},{5,4},{6,7},{7,6},{8,9},{9,8},{10,11... | collective-permute-start | bytes 3145736 | tf_op jit(solution)/shard_map/ppermute | solution.py:31
  152.8 9.2 %collective-permute-start.15 = (f32[8,2,256]{2,1,0:T(2,128)S(1)}, f32[8,2,256]{2,1,0:T(2,128)S(1)}, u32[]{:S(2)}, u32[]{:S(2)}) collective-permute-start(f32[8,2,256]{2,1,0:T(2,128)S(1)} %copy-done.12), channel_id=1, source_target_pairs={{1,0},{3,2},{4,1},{5,4},{6,3},{7,6},{8,5},{9,8},{10,7},{11,10},{12... | collective-permute-start | bytes 49160 | tf_op jit(solution)/shard_map/ppermute | solution.py:31
  154.8 7.3 %collective-permute-start.16 = (f32[8,2,256]{2,1,0:T(2,128)S(1)}, f32[8,2,256]{2,1,0:T(2,128)S(1)}, u32[]{:S(2)}, u32[]{:S(2)}) collective-permute-start(f32[8,2,256]{2,1,0:T(2,128)S(1)} %copy-done.12), channel_id=1, source_target_pairs={{2,0},{3,1},{4,2},{5,3},{6,4},{7,5},{8,6},{9,7},{10,8},{11,9},{12,... | collective-permute-start | bytes 49160 | tf_op jit(solution)/shard_map/ppermute | solution.py:31
  159.5 5.5 %collective-permute-start.17 = (f32[8,2,256]{2,1,0:T(2,128)S(1)}, f32[8,2,256]{2,1,0:T(2,128)S(1)}, u32[]{:S(2)}, u32[]{:S(2)}) collective-permute-start(f32[8,2,256]{2,1,0:T(2,128)S(1)} %copy-done.12), channel_id=1, source_target_pairs={{2,1},{3,0},{4,3},{5,2},{6,5},{7,4},{8,7},{9,6},{10,9},{11,8},{12,... | collective-permute-start | bytes 49160 | tf_op jit(solution)/shard_map/ppermute | solution.py:31
  162.0 3.0 %copy-start.8 = (f32[8,2,256]{2,1,0:T(2,128)}, f32[8,2,256]{2,1,0:T(2,128)S(1)}, u32[]{:S(2)}) copy-start(f32[8,2,256]{2,1,0:T(2,128)S(1)} %collective-permute-done.15.refs_13_) | copy-start | bytes 49156
  162.1 3.0 %copy-start.9 = (f32[8,2,256]{2,1,0:T(2,128)}, f32[8,2,256]{2,1,0:T(2,128)S(1)}, u32[]{:S(2)}) copy-start(f32[8,2,256]{2,1,0:T(2,128)S(1)} %collective-permute-done.16.refs_14_) | copy-start | bytes 49156
  165.0 0.6 copy-start.11
  165.0 1.0 copy-start.4
